TPU v7x, 32 devices: a whole 2x2x4 slice. The times are simulated.
32 devices in a mesh: member: 8 (over z, y), band: 4 (over x, core).
Axes of the slice: x: 2, y: 2, z: 4, core: 2. Of those that a mesh axis runs over, the one named last changes fastest.
Arguments:
- spectral: float32 [128, 768, 768], P('member', 'band'), parts along dimension 0, may hold values from -6 to 6
- coupling: float32 [8192, 1024], P(('member', 'band')), parts along dimension 0, may hold values from 0.02 to 162, as said below
- quadratic: float32 [8192, 1024], P(('member', 'band')), parts along dimension 0, may hold values from -1.5 to 1.5
Outputs:
- tendency_spectral: float32 [128, 768, 768], P('member', 'band'), parts along dimension 0
There are 8 independent parts, one for each index of `member`. A program takes and returns all parts, laid end to end along the dimension named above; each array names one. Nothing has to cross between parts.
Inputs may be any that keep to these rules, and one draw needn't show every extreme that they name: `coupling`: positive.
All inputs are finite; a program needn't handle non-finite values.
Results may differ from a plain program's by a relative error of at most 0.00008.
Values sent between devices are 32-bit elements; how exact they have to be, the bound alone decides.
A program may use at most 128 MiB of HBM per device.

v0:
```python
import math

import jax
import jax.numpy as jnp
from jax import lax
from jax.sharding import PartitionSpec as P


def tables(cells, coeffs):
    half_count = coeffs // 2
    position = jnp.arange(cells, dtype=jnp.int32)
    column = jnp.arange(coeffs, dtype=jnp.int32)
    wavenumber = jnp.where(column < half_count, column, column - half_count)
    turns = position[:, None] * wavenumber[None, :] % cells
    angles = turns.astype(jnp.float32) * (2.0 * math.pi / cells)
    basis_table = jnp.where(column[None, :] < half_count, jnp.cos(angles), jnp.sin(angles))
    synthesis = basis_table / math.sqrt(half_count)
    factor = jnp.where(wavenumber == 0, 1.0, 2.0) * (math.sqrt(half_count) / cells)
    analysis = (basis_table * factor[None, :]).T
    return (synthesis, analysis)


def on_device(spectral, coupling, quadratic):
    high = lax.Precision.HIGHEST
    coeffs = spectral.shape[2]
    cells = coupling.shape[1]
    synthesis, analysis = tables(cells, coeffs)
    points = float(cells * cells)
    section = jnp.einsum("lab,yb->lay", spectral, synthesis, precision=high)
    turned = lax.all_to_all(section, "band", split_axis=2, concat_axis=1, tiled=True)
    grid = jnp.einsum("xa,lay->lyx", synthesis, turned, precision=high)
    product = coupling[None] * grid
    product, local_sum = (product, jnp.sum(product * product, axis=(1, 2)))
    total = lax.psum(local_sum, "band")
    scaled = product / jnp.sqrt(total / points + 1e-06)[:, None, None]
    tendency = scaled + quadratic[None] * scaled * scaled
    back = jnp.einsum("ax,lyx->lya", analysis, tendency, precision=high)
    returned = lax.all_to_all(back, "band", split_axis=2, concat_axis=1, tiled=True)
    return jnp.einsum("by,lya->lab", analysis, returned, precision=high)


def solution(mesh):
    placed = (P("member", "band", None), P(("member", "band"), None), P(("member", "band"), None))
    return jax.shard_map(
        on_device, mesh=mesh, in_specs=placed, out_specs=P("member", "band", None), check_vma=False
    )
```

profile of v0, /device:TPU:0, one launch (start us, length us, event | category | flops | bytes accessed | tf_op | source)
XLA Modules:
  0.0 669.1 jit_solution(13568946825027268618)
XLA Ops:
  0.0 12.7 %fusion.59 = f32[1024,768,1]{1,0,2:T(8,128)S(1)} fusion(s32[768]{0:T(1024)S(1)} %add_select_fusion.1, pred[768]{0:T(1024)(128)(4,1)S(1)} %iota_compare_fusion), kind=kLoop, calls=%fused_computation.20.clone.1 | loop fusion | flops 12582912 | bytes 3149568 | tf_op jit(solution)/shard_map/lab,yb->lay/dot_general | solution.py:29
  12.7 34.2 %convolution_bitcast_fusion = f32[16,192,1024]{2,1,0:T(8,128)} fusion(f32[16,192,768]{2,1,0:T(8,128)} %param.3, f32[1024,768,1]{1,0,2:T(8,128)S(1)} %fusion.59), kind=kOutput, calls=%fused_computation.11 | convolution fusion | flops 28991029248 | bytes 25165824 | tf_op jit(solution)/shard_map/lab,yb->lay/dot_general | solution.py:29
  46.9 17.7 %copy.15 = f32[16,192,1024]{1,0,2:T(8,128)} copy(f32[16,192,1024]{2,1,0:T(8,128)} %convolution_bitcast_fusion) | data formatting | bytes 25165824 | tf_op jit(solution)/shard_map/lab,yb->lay/dot_general | solution.py:29
  64.6 18.3 %all-to-all-start = ((f32[16,192,1024]{1,0,2:T(8,128)}), f32[16,192,1024]{1,0,2:T(8,128)}, u32[]{:S(2)}, u32[]{:S(2)}) async-start(f32[16,192,1024]{1,0,2:T(8,128)} %copy.15), calls=%async_computation | async-start | bytes 33554432 | tf_op jit(solution)/shard_map/all_to_all | solution.py:30
  83.0 12.4 %fusion.13.clone.4 = f32[1024,768,1]{1,0,2:T(8,128)S(1)} fusion(s32[768]{0:T(1024)S(1)} %add_select_fusion.1, pred[768]{0:T(1024)(128)(4,1)S(1)} %iota_compare_fusion), kind=kLoop, calls=%fused_computation.19.clone.clone.clone.1 | loop fusion | flops 12582912 | bytes 3149568 | tf_op jit(solution)/shard_map/reduce_sum | solution.py:33
  95.4 159.9 %all-to-all-done = f32[16,192,1024]{1,0,2:T(8,128)} async-done(((f32[16,192,1024]{1,0,2:T(8,128)}), f32[16,192,1024]{1,0,2:T(8,128)}, u32[]{:S(2)}, u32[]{:S(2)}) %all-to-all-start) | async-done | bytes 12582944 | tf_op jit(solution)/shard_map/all_to_all | solution.py:30
  255.3 14.5 %copy.23 = f32[16,192,4,256]{3,2,1,0:T(4,128)} copy(f32[16,192,4,256]{1,0,3,2:T(8,128)} %bitcast.2) | data formatting | bytes 25165824 | tf_op jit(solution)/shard_map/all_to_all | solution.py:30
  269.8 0.0 copy-start
  269.8 11.3 %copy.17 = f32[16,4,192,256]{3,2,1,0:T(8,128)} copy(f32[16,4,192,256]{3,1,2,0:T(4,128)} %bitcast.45) | data formatting | bytes 25165824 | tf_op jit(solution)/shard_map/all_to_all | solution.py:30
  281.1 0.0 copy-done
  281.1 83.8 %multiply_reduce_fusion = (f32[16]{0:T(128)S(1)}, f32[16,256,1024]{2,1,0:T(8,128)}) fusion(f32[256,1024]{1,0:T(8,128)S(1)} %copy-done, f32[16,768,256]{2,1,0:T(8,128)} %bitcast.46, f32[1024,768,1]{1,0,2:T(8,128)S(1)} %fusion.13.clone.4), kind=kOutput, calls=%fused_computation.3 | convolution fusion | flops 38667288576 | bytes 33554496 | tf_op jit(solution)/shard_map/xa,lay->lyx/dot_general | solution.py:31
  365.0 5.8 psum.7
  370.7 12.9 %multiply_add_fusion.5 = f32[16,256,1024]{2,1,0:T(8,128)} fusion(f32[16,256,1024]{2,1,0:T(8,128)} %get-tuple-element.6, f32[256,1024]{1,0:T(8,128)} %param.5, f32[16]{0:T(128)S(1)} %add_sqrt_fusion, f32[256,1024]{1,0:T(8,128)} %param.4), kind=kLoop, calls=%fused_computation.clone.clone.2 | loop fusion | flops 20971520 | bytes 35651648 | tf_op jit(solution)/shard_map/ax,lyx->lya/dot_general | solution.py:37
  383.7 58.5 %fusion = f32[16,256,768]{2,1,0:T(8,128)} fusion(f32[768]{0:T(1024)S(1)} %select_multiply_fusion, s32[768]{0:T(1024)S(1)} %add_select_fusion.1, pred[768]{0:T(1024)(128)(4,1)S(1)} %iota_compare_fusion, f32[16,256,1024]{2,1,0:T(8,128)} %multiply_add_fusion.5), kind=kOutput, calls=%fused_computation.1 | convolution fusion | flops 38667288576 | bytes 29367040 | tf_op jit(solution)/shard_map/ax,lyx->lya/dot_general | solution.py:37
  442.2 12.8 %copy.19 = f32[16,256,768]{1,0,2:T(8,128)} copy(f32[16,256,768]{2,1,0:T(8,128)} %fusion) | data formatting | bytes 25165824 | tf_op jit(solution)/shard_map/ax,lyx->lya/dot_general | solution.py:37
  455.0 6.5 all-to-all-start.1
  461.5 12.7 %fusion.61 = f32[1024,768,1]{1,0,2:T(8,128)S(1)} fusion(f32[768]{0:T(1024)S(1)} %select_multiply_fusion, s32[768]{0:T(1024)S(1)} %add_select_fusion.1, pred[768]{0:T(1024)(128)(4,1)S(1)} %iota_compare_fusion), kind=kLoop, calls=%fused_computation.16.clone.1 | loop fusion | flops 12582912 | bytes 3152640 | tf_op jit(solution)/shard_map/by,lya->lab/dot_general | solution.py:39
  474.2 125.2 %all-to-all-done.1 = f32[16,256,768]{1,0,2:T(8,128)} async-done(((f32[16,256,768]{1,0,2:T(8,128)}), f32[16,256,768]{1,0,2:T(8,128)}, u32[]{:S(2)}, u32[]{:S(2)}) %all-to-all-start.1) | async-done | bytes 12582944 | tf_op jit(solution)/shard_map/all_to_all | solution.py:38
  599.4 16.5 %copy.21 = f32[16,4,256,192]{2,1,3,0:T(4,128)} copy(f32[16,4,256,192]{2,0,3,1:T(8,128)} %bitcast.8) | data formatting | bytes 25165824 | tf_op jit(solution)/shard_map/all_to_all | solution.py:38
  615.9 15.7 %all_to_all.33 = f32[16,1024,192]{1,2,0:T(8,128)} reshape(f32[16,4,256,192]{2,1,3,0:T(4,128)} %copy.21) | data formatting | bytes 25165824 | tf_op jit(solution)/shard_map/all_to_all | solution.py:38
  631.6 37.1 %fusion.9 = f32[16,192,768]{2,1,0:T(8,128)} fusion(f32[16,1024,192]{1,2,0:T(8,128)} %all_to_all.33, f32[1024,768,1]{1,0,2:T(8,128)S(1)} %fusion.61), kind=kOutput, calls=%fused_computation.15 | convolution fusion | flops 28991029248 | bytes 25165824 | tf_op jit(solution)/shard_map/by,lya->lab/dot_general | solution.py:39
  (4 shorter events, 0.0 us)
Async XLA Ops:
  64.6 190.7 %all-to-all-start = ((f32[16,192,1024]{1,0,2:T(8,128)}), f32[16,192,1024]{1,0,2:T(8,128)}, u32[]{:S(2)}, u32[]{:S(2)}) async-start(f32[16,192,1024]{1,0,2:T(8,128)} %copy.15), calls=%async_computation | async-start | bytes 33554432 | tf_op jit(solution)/shard_map/all_to_all | solution.py:30
  269.8 11.3 %copy-start = (f32[256,1024]{1,0:T(8,128)S(1)}, f32[256,1024]{1,0:T(8,128)}, u32[]{:S(2)}) copy-start(f32[256,1024]{1,0:T(8,128)} %param.4) | copy-start | bytes 3145732
  455.0 144.4 %all-to-all-start.1 = ((f32[16,256,768]{1,0,2:T(8,128)}), f32[16,256,768]{1,0,2:T(8,128)}, u32[]{:S(2)}, u32[]{:S(2)}) async-start(f32[16,256,768]{1,0,2:T(8,128)} %copy.19), calls=%async_computation.1 | async-start | bytes 25165824 | tf_op jit(solution)/shard_map/all_to_all | solution.py:38
where the time goes:
time: 679 us; the launch traced here: 669 us
  waiting for transfers between devices  285 us (42%)
  matrix products  214 us (32%)
  local copies, waits for them, and re-layouts  88.5 us (13%)
  other arithmetic  50.8 us (7%)
  starting transfers between devices  24.9 us (4%)
    all_to_all x1, waiting for transfers between devices, on_device(): lax.all_to_all(section, 'band', split_axis=2, concat_axis=1, tiled=True)  160 us
    all_to_all x1, waiting for transfers between devices, on_device(): lax.all_to_all(back, 'band', split_axis=2, concat_axis=1, tiled=True)  125 us
    dot_general x1, matrix products, on_device(): grid = jnp.einsum('xa,lay->lyx', synthesis, turned, precision=high)  83.8 us
    dot_general x1, matrix products, on_device(): back = jnp.einsum('ax,lyx->lya', analysis, tendency, precision=high)  58.5 us
    dot_general x1, matrix products, on_device(): return jnp.einsum('by,lya->lab', analysis, returned, precision=high)  37.1 us
    dot_general x1, matrix products, on_device(): section = jnp.einsum('lab,yb->lay', spectral, synthesis, precision=high)  34.2 us
    all_to_all x2, local copies, waits for them, and re-layouts, on_device(): lax.all_to_all(back, 'band', split_axis=2, concat_axis=1, tiled=True)  32.2 us
    all_to_all x2, local copies, waits for them, and re-layouts, on_device(): lax.all_to_all(section, 'band', split_axis=2, concat_axis=1, tiled=True)  25.8 us
  transfers between devices with their start and end apart: 2, of which 2 were waited for; matrix products, arithmetic and copies ran while one was open for 4% of the time, Pallas kernels for 0%

commit v1 on v0

--- a/solution.py
+++ b/solution.py
@@ -21,22 +21,33 @@
 
 
 def on_device(spectral, coupling, quadratic):
-    high = lax.Precision.HIGHEST
-    coeffs = spectral.shape[2]
+    high = lax.Precision.HIGH
+    levels, band, coeffs = spectral.shape
     cells = coupling.shape[1]
+    ways = lax.axis_size("band")
     synthesis, analysis = tables(cells, coeffs)
     points = float(cells * cells)
-    section = jnp.einsum("lab,yb->lay", spectral, synthesis, precision=high)
-    turned = lax.all_to_all(section, "band", split_axis=2, concat_axis=1, tiled=True)
-    grid = jnp.einsum("xa,lay->lyx", synthesis, turned, precision=high)
-    product = coupling[None] * grid
-    product, local_sum = (product, jnp.sum(product * product, axis=(1, 2)))
-    total = lax.psum(local_sum, "band")
-    scaled = product / jnp.sqrt(total / points + 1e-06)[:, None, None]
-    tendency = scaled + quadratic[None] * scaled * scaled
-    back = jnp.einsum("ax,lyx->lya", analysis, tendency, precision=high)
-    returned = lax.all_to_all(back, "band", split_axis=2, concat_axis=1, tiled=True)
-    return jnp.einsum("by,lya->lab", analysis, returned, precision=high)
+
+    arrived = [
+        lax.all_to_all(spectral[at : at + ways], "band", split_axis=0, concat_axis=0, tiled=True)
+        for at in range(0, levels, ways)
+    ]
+    coupling = lax.all_gather(coupling, "band", axis=0, tiled=True)
+    quadratic = lax.all_gather(quadratic, "band", axis=0, tiled=True)
+    outputs = []
+    for field in arrived:
+        field = field.reshape(coeffs, coeffs)
+        section = jnp.einsum("xa,ab->xb", synthesis, field, precision=high)
+        grid = jnp.einsum("yb,xb->yx", synthesis, section, precision=high)
+        product = coupling * grid
+        energy = jnp.sum(product * product) / points
+        scaled = product * (1.0 / jnp.sqrt(energy + 1e-06))
+        tendency = scaled + quadratic * scaled * scaled
+        back = jnp.einsum("ax,yx->ay", analysis, tendency, precision=high)
+        done = jnp.einsum("ay,by->ab", back, analysis, precision=high)
+        done = done.reshape(ways, band, coeffs)
+        outputs.append(lax.all_to_all(done, "band", split_axis=0, concat_axis=0, tiled=True))
+    return jnp.concatenate(outputs, axis=0)
 
 
 def solution(mesh):

time: 679 us -> 566 us (0.83)
  waiting for transfers between devices: 285 us -> 72.4 us
  matrix products: 214 us -> 342 us
  local copies, waits for them, and re-layouts: 88.5 us -> 6.85 us
  blocking collectives: 5.76 us -> 87 us
  other arithmetic: 50.8 us -> 6.19 us
  between operations: 0.49 us -> 16.8 us
    all_to_all x2 -> x6, waiting for transfers between devices: 285 us -> 71 us  [the longest x3 71 us: on_device(): lax.all_to_all(spectral[at:at + ways], 'band', split_axis=0, concat_axis=...]
    dot_general x4 -> x16, matrix products: 214 us -> 342 us  [the longest x4 105 us: on_device(): back = jnp.einsum('ax,yx->ay', analysis, tendency, precision=high)]
    all_to_all x0 -> x2, blocking collectives: none -> 87 us  [the longest x1 55 us: on_device(): lax.all_to_all(spectral[at:at + ways], 'band', split_axis=0, concat_axis=...]
    all_to_all x4 -> x0, local copies, waits for them, and re-layouts: 58 us -> none  [the longest x2 32.2 us: on_device(): lax.all_to_all(back, 'band', split_axis=2, concat_axis=1, tiled=True)]
    dot_general x3 -> x0, other arithmetic: 38.3 us -> none  [the longest x1 12.9 us: on_device(): back = jnp.einsum('ax,lyx->lya', analysis, tendency, precision=high)]
    dot_general x2 -> x0, local copies, waits for them, and re-layouts: 30.5 us -> none  [the longest x1 17.7 us: on_device(): section = jnp.einsum('lab,yb->lay', spectral, synthesis, precision=high)]
    reduce_sum x1 -> x0, other arithmetic: 12.4 us -> none  [on_device(): product, local_sum = (product, jnp.sum(product * product, axis=(1, 2)))]
    slice x0 -> x1, local copies, waits for them, and re-layouts: none -> 6.85 us  [on_device(): spectral[at:at + ways]]
  transfers between devices with their start and end apart: 2 -> 8, of which waited for: 2 -> 2; matrix products, arithmetic and copies ran while one was open for 4% -> 55% of each run, Pallas kernels for 0% -> 0%
where the time goes in v1:
time: 566 us; the launch traced here: 557 us
  matrix products  342 us (60%)
  blocking collectives  87 us (15%)
  waiting for transfers between devices  72.4 us (13%)
  starting transfers between devices  26.2 us (5%)
  between operations  16.8 us (3%)
  local copies, waits for them, and re-layouts  6.85 us (1%)
  other arithmetic  6.19 us (1%)
    dot_general x4, matrix products, on_device(): back = jnp.einsum('ax,yx->ay', analysis, tendency, precision=high)  105 us
    dot_general x4, matrix products, on_device(): grid = jnp.einsum('yb,xb->yx', synthesis, section, precision=high)  88.9 us
    dot_general x4, matrix products, on_device(): section = jnp.einsum('xa,ab->xb', synthesis, field, precision=high)  76.7 us
    dot_general x4, matrix products, on_device(): done = jnp.einsum('ay,by->ab', back, analysis, precision=high)  71 us
    all_to_all x3, waiting for transfers between devices, on_device(): lax.all_to_all(spectral[at:at + ways], 'band', split_axis=0, concat_axis=...  71 us
    all_to_all x1, blocking collectives, on_device(): lax.all_to_all(spectral[at:at + ways], 'band', split_axis=0, concat_axis=...  55 us
    all_to_all x1, blocking collectives, on_device(): lax.all_to_all(done, 'band', split_axis=0, concat_axis=0, tiled=True)  32.1 us
    all_to_all x3, starting transfers between devices, on_device(): lax.all_to_all(spectral[at:at + ways], 'band', split_axis=0, concat_axis=...  13.5 us
  transfers between devices with their start and end apart: 8, of which 2 were waited for; matrix products, arithmetic and copies ran while one was open for 55% of the time, Pallas kernels for 0%

profile of v1, /device:TPU:0, one launch (start us, length us, event | category | flops | bytes accessed | tf_op | source)
XLA Modules:
  0.0 557.4 jit_solution(15243473083543496365)
XLA Ops:
  6.5 0.7 all-gather.3.cloned.1.call-update
  7.3 6.8 %fusion.130 = (f32[4,192,768]{2,1,0:T(8,128)S(1)}, f32[4,192,768]{2,1,0:T(8,128)}, f32[4,192,768]{2,1,0:T(8,128)}, f32[4,192,768]{2,1,0:T(8,128)}) fusion(f32[16,192,768]{2,1,0:T(8,128)} %param.3), kind=kLoop, calls=%fused_computation.150 | loop fusion | bytes 18874368 | tf_op jit(solution)/shard_map/slice | solution.py:32
  14.1 55.0 %all_to_all.40 = f32[4,192,768]{2,1,0:T(8,128)S(1)} all-to-all(f32[4,192,768]{2,1,0:T(8,128)S(1)} %get-tuple-element.5), channel_id=1, replica_groups=mesh['member'=8,'band'=4] {'band'}, dimensions={0} | all-to-all | bytes 4718592 | tf_op jit(solution)/shard_map/all_to_all | solution.py:32
  69.1 4.5 all-to-all-start.2
  73.6 0.0 all-gather.5.cloned.1.call-start
  73.6 0.7 all-gather.5.cloned.1.call-update
  74.3 42.2 %all-to-all-done.2 = f32[4,192,768]{2,1,0:T(8,128)} async-done(((f32[4,192,768]{2,1,0:T(8,128)}), f32[4,192,768]{2,1,0:T(8,128)}, u32[]{:S(2)}, u32[]{:S(2)}) %all-to-all-start.2) | async-done | bytes 2359328 | tf_op jit(solution)/shard_map/all_to_all | solution.py:32
  116.6 4.5 all-to-all-start.4
  121.1 28.7 %all-to-all-done.4 = f32[4,192,768]{2,1,0:T(8,128)} async-done(((f32[4,192,768]{2,1,0:T(8,128)}), f32[4,192,768]{2,1,0:T(8,128)}, u32[]{:S(2)}, u32[]{:S(2)}) %all-to-all-start.4) | async-done | bytes 2359328 | tf_op jit(solution)/shard_map/all_to_all | solution.py:32
  149.9 4.5 all-to-all-start.6
  154.4 17.8 %fusion.28 = f32[1024,768]{1,0:T(8,128)} fusion(f32[768,768]{1,0:T(8,128)S(1)} %bitcast.20, s32[768]{0:T(1024)S(1)} %add_select_fusion.1, pred[768]{0:T(1024)(128)(4,1)S(1)} %iota_compare_fusion), kind=kOutput, calls=%fused_computation.45 | convolution fusion | flops 3636461568 | bytes 5508864 | tf_op jit(solution)/shard_map/xa,ab->xb/dot_general | solution.py:40
  172.2 19.6 %fusion.25 = f32[1024,768]{1,0:T(8,128)} fusion(f32[768,768]{1,0:T(8,128)} %bitcast.2, s32[768]{0:T(1024)S(1)} %add_select_fusion.1, pred[768]{0:T(1024)(128)(4,1)S(1)} %iota_compare_fusion), kind=kOutput, calls=%fused_computation.42 | convolution fusion | flops 3636461568 | bytes 5508864 | tf_op jit(solution)/shard_map/xa,ab->xb/dot_general | solution.py:40
  191.7 19.8 %fusion.22 = f32[1024,768]{1,0:T(8,128)} fusion(f32[768,768]{1,0:T(8,128)} %bitcast.4, s32[768]{0:T(1024)S(1)} %add_select_fusion.1, pred[768]{0:T(1024)(128)(4,1)S(1)} %iota_compare_fusion), kind=kOutput, calls=%fused_computation.39 | convolution fusion | flops 3636461568 | bytes 5508864 | tf_op jit(solution)/shard_map/xa,ab->xb/dot_general | solution.py:40
  211.5 19.5 %fusion.19 = f32[1024,768]{1,0:T(8,128)} fusion(f32[768,768]{1,0:T(8,128)} %bitcast.6, s32[768]{0:T(1024)S(1)} %add_select_fusion.1, pred[768]{0:T(1024)(128)(4,1)S(1)} %iota_compare_fusion), kind=kOutput, calls=%fused_computation.36 | convolution fusion | flops 3636461568 | bytes 5508864 | tf_op jit(solution)/shard_map/xa,ab->xb/dot_general | solution.py:40
  231.1 22.2 %multiply_reduce_fusion.3 = (f32[]{:T(128)}, f32[1024,1024]{1,0:T(8,128)}) fusion(f32[1024,1024]{1,0:T(8,128)} %all-gather.3.cloned.1.call-done, f32[1024,768]{1,0:T(8,128)} %fusion.28, s32[768]{0:T(1024)S(1)} %add_select_fusion.1, pred[768]{0:T(1024)(128)(4,1)S(1)} %iota_compare_fusion), kind=kOutput, calls=%fused_computation.19 | convolution fusion | flops 4847566848 | bytes 11538180 | tf_op jit(solution)/shard_map/yb,xb->yx/dot_general | solution.py:41
  254.0 0.0 all-gather.5.cloned.1.call-done
  254.1 26.3 %fusion = f32[768,1024]{1,0:T(8,128)S(1)} fusion(f32[1024,1024]{1,0:T(8,128)} %all-gather.5.cloned.1.call-done, f32[1024,1024]{1,0:T(8,128)} %get-tuple-element.16, f32[]{:T(128)S(6)} %sqrt.12, f32[768]{0:T(1024)S(1)} %select_multiply_fusion, s32[768]{0:T(1024)S(1)} %add_select_fusion.1, pred[768]{0:T(1024)(128)(4,1)S(1)} %iota_compare_fusion), kind=kOutput, calls=%fused_computation.8 | convolution fusion | flops 4848615424 | bytes 11541252 | tf_op jit(solution)/shard_map/ax,yx->ay/dot_general | solution.py:46
  280.4 17.9 %fusion.39 = f32[768,768]{1,0:T(8,128)} fusion(f32[768,1024]{1,0:T(8,128)S(1)} %fusion, f32[768]{0:T(1024)S(1)} %select_multiply_fusion, s32[768]{0:T(1024)S(1)} %add_select_fusion.1, pred[768]{0:T(1024)(128)(4,1)S(1)} %iota_compare_fusion), kind=kOutput, calls=%fused_computation.56 | convolution fusion | flops 3636461568 | bytes 5511936 | tf_op jit(solution)/shard_map/ay,by->ab/dot_general | solution.py:47
  298.3 3.6 all-to-all-start.1
  301.9 22.2 %multiply_reduce_fusion.2 = (f32[]{:T(128)}, f32[1024,1024]{1,0:T(8,128)}) fusion(f32[1024,1024]{1,0:T(8,128)} %all-gather.3.cloned.1.call-done, f32[1024,768]{1,0:T(8,128)} %fusion.25, s32[768]{0:T(1024)S(1)} %add_select_fusion.1, pred[768]{0:T(1024)(128)(4,1)S(1)} %iota_compare_fusion), kind=kOutput, calls=%fused_computation.17 | convolution fusion | flops 4847566848 | bytes 11538180 | tf_op jit(solution)/shard_map/yb,xb->yx/dot_general | solution.py:41
  324.9 26.2 %fusion.1 = f32[768,1024]{1,0:T(8,128)S(1)} fusion(f32[1024,1024]{1,0:T(8,128)} %all-gather.5.cloned.1.call-done, f32[1024,1024]{1,0:T(8,128)} %get-tuple-element.14, f32[]{:T(128)S(6)} %sqrt.13, f32[768]{0:T(1024)S(1)} %select_multiply_fusion, s32[768]{0:T(1024)S(1)} %add_select_fusion.1, pred[768]{0:T(1024)(128)(4,1)S(1)} %iota_compare_fusion), kind=kOutput, calls=%fused_computation.9 | convolution fusion | flops 4848615424 | bytes 11541252 | tf_op jit(solution)/shard_map/ax,yx->ay/dot_general | solution.py:46
  351.1 17.8 %fusion.36 = f32[768,768]{1,0:T(8,128)} fusion(f32[768,1024]{1,0:T(8,128)S(1)} %fusion.1, f32[768]{0:T(1024)S(1)} %select_multiply_fusion, s32[768]{0:T(1024)S(1)} %add_select_fusion.1, pred[768]{0:T(1024)(128)(4,1)S(1)} %iota_compare_fusion), kind=kOutput, calls=%fused_computation.53 | convolution fusion | flops 3636461568 | bytes 5511936 | tf_op jit(solution)/shard_map/ay,by->ab/dot_general | solution.py:47
  368.9 4.5 all-to-all-start.3
  373.4 22.2 %multiply_reduce_fusion.1 = (f32[]{:T(128)}, f32[1024,1024]{1,0:T(8,128)}) fusion(f32[1024,1024]{1,0:T(8,128)} %all-gather.3.cloned.1.call-done, f32[1024,768]{1,0:T(8,128)} %fusion.22, s32[768]{0:T(1024)S(1)} %add_select_fusion.1, pred[768]{0:T(1024)(128)(4,1)S(1)} %iota_compare_fusion), kind=kOutput, calls=%fused_computation.15 | convolution fusion | flops 4847566848 | bytes 11538180 | tf_op jit(solution)/shard_map/yb,xb->yx/dot_general | solution.py:41
  396.4 26.5 %fusion.2 = f32[768,1024]{1,0:T(8,128)S(1)} fusion(f32[1024,1024]{1,0:T(8,128)} %all-gather.5.cloned.1.call-done, f32[1024,1024]{1,0:T(8,128)} %get-tuple-element.12, f32[]{:T(128)S(6)} %sqrt.14, f32[768]{0:T(1024)S(1)} %select_multiply_fusion, s32[768]{0:T(1024)S(1)} %add_select_fusion.1, pred[768]{0:T(1024)(128)(4,1)S(1)} %iota_compare_fusion), kind=kOutput, calls=%fused_computation.10 | convolution fusion | flops 4848615424 | bytes 11541252 | tf_op jit(solution)/shard_map/ax,yx->ay/dot_general | solution.py:46
  422.9 17.7 %fusion.33 = f32[768,768]{1,0:T(8,128)} fusion(f32[768,1024]{1,0:T(8,128)S(1)} %fusion.2, f32[768]{0:T(1024)S(1)} %select_multiply_fusion, s32[768]{0:T(1024)S(1)} %add_select_fusion.1, pred[768]{0:T(1024)(128)(4,1)S(1)} %iota_compare_fusion), kind=kOutput, calls=%fused_computation.50 | convolution fusion | flops 3636461568 | bytes 5511936 | tf_op jit(solution)/shard_map/ay,by->ab/dot_general | solution.py:47
  440.5 4.5 all-to-all-start.5
  445.0 22.2 %multiply_reduce_fusion = (f32[]{:T(128)}, f32[1024,1024]{1,0:T(8,128)}) fusion(f32[1024,1024]{1,0:T(8,128)} %all-gather.3.cloned.1.call-done, f32[1024,768]{1,0:T(8,128)} %fusion.19, s32[768]{0:T(1024)S(1)} %add_select_fusion.1, pred[768]{0:T(1024)(128)(4,1)S(1)} %iota_compare_fusion), kind=kOutput, calls=%fused_computation.13 | convolution fusion | flops 4847566848 | bytes 11538180 | tf_op jit(solution)/shard_map/yb,xb->yx/dot_general | solution.py:41
  467.9 26.3 %fusion.3 = f32[768,1024]{1,0:T(8,128)S(1)} fusion(f32[1024,1024]{1,0:T(8,128)} %all-gather.5.cloned.1.call-done, f32[1024,1024]{1,0:T(8,128)} %get-tuple-element.10, f32[]{:T(128)S(6)} %sqrt.15, f32[768]{0:T(1024)S(1)} %select_multiply_fusion, s32[768]{0:T(1024)S(1)} %add_select_fusion.1, pred[768]{0:T(1024)(128)(4,1)S(1)} %iota_compare_fusion), kind=kOutput, calls=%fused_computation.11 | convolution fusion | flops 4848615424 | bytes 11541252 | tf_op jit(solution)/shard_map/ax,yx->ay/dot_general | solution.py:46
  494.2 17.7 %fusion.30 = f32[768,768]{1,0:T(8,128)} fusion(f32[768,1024]{1,0:T(8,128)S(1)} %fusion.3, f32[768]{0:T(1024)S(1)} %select_multiply_fusion, s32[768]{0:T(1024)S(1)} %add_select_fusion.1, pred[768]{0:T(1024)(128)(4,1)S(1)} %iota_compare_fusion), kind=kOutput, calls=%fused_computation.47 | convolution fusion | flops 3636461568 | bytes 5511936 | tf_op jit(solution)/shard_map/ay,by->ab/dot_general | solution.py:47
  511.9 32.1 %all_to_all.41 = f32[4,192,768]{2,1,0:T(8,128)S(1)} all-to-all(f32[4,192,768]{2,1,0:T(8,128)} %bitcast.24), channel_id=1, replica_groups=mesh['member'=8,'band'=4] {'band'}, dimensions={0} | all-to-all | bytes 4718592 | tf_op jit(solution)/shard_map/all_to_all | solution.py:49
  544.0 6.2 %pad_maximum_fusion = f32[16,192,768]{2,1,0:T(8,128)} fusion(f32[4,192,768]{2,1,0:T(8,128)S(1)} %all_to_all.41, f32[4,192,768]{2,1,0:T(8,128)} %all-to-all-done.5, f32[4,192,768]{2,1,0:T(8,128)} %all-to-all-done.3, f32[4,192,768]{2,1,0:T(8,128)S(1)} %all-to-all-done.1), kind=kLoop, calls=%fused_computation | loop fusion | flops 7077888 | bytes 18874368 | tf_op jit(solution)/shard_map/concatenate | solution.py:50
  (9 shorter events, 0.0 us)
Async XLA Ops:
  6.5 224.5 %all-gather.3.cloned.1.call-start = ((), (), s32[]{:S(2)}) async-start(), calls=%async_computation.8 | async-start | bytes 5242880 | tf_op jit(solution)/shard_map/all_gather | solution.py:35
  69.1 47.5 %all-to-all-start.2 = ((f32[4,192,768]{2,1,0:T(8,128)}), f32[4,192,768]{2,1,0:T(8,128)}, u32[]{:S(2)}, u32[]{:S(2)}) async-start(f32[4,192,768]{2,1,0:T(8,128)} %get-tuple-element.6), calls=%async_computation.2 | async-start | bytes 4718592 | tf_op jit(solution)/shard_map/all_to_all | solution.py:32
  73.6 180.5 %all-gather.5.cloned.1.call-start = ((), (), s32[]{:S(2)}) async-start(), calls=%async_computation.9 | async-start | bytes 5242880 | tf_op jit(solution)/shard_map/all_gather | solution.py:36
  116.6 33.3 %all-to-all-start.4 = ((f32[4,192,768]{2,1,0:T(8,128)}), f32[4,192,768]{2,1,0:T(8,128)}, u32[]{:S(2)}, u32[]{:S(2)}) async-start(f32[4,192,768]{2,1,0:T(8,128)} %get-tuple-element.8), calls=%async_computation.4 | async-start | bytes 4718592 | tf_op jit(solution)/shard_map/all_to_all | solution.py:32
  149.9 61.6 %all-to-all-start.6 = ((f32[4,192,768]{2,1,0:T(8,128)}), f32[4,192,768]{2,1,0:T(8,128)}, u32[]{:S(2)}, u32[]{:S(2)}) async-start(f32[4,192,768]{2,1,0:T(8,128)} %get-tuple-element.7), calls=%async_computation.6 | async-start | bytes 4718592 | tf_op jit(solution)/shard_map/all_to_all | solution.py:32
  298.3 70.6 %all-to-all-start.1 = ((f32[4,192,768]{2,1,0:T(8,128)}), f32[4,192,768]{2,1,0:T(8,128)S(1)}, u32[]{:S(2)}, u32[]{:S(2)}) async-start(f32[4,192,768]{2,1,0:T(8,128)} %bitcast.23), calls=%async_computation.1 | async-start | bytes 4718592 | tf_op jit(solution)/shard_map/all_to_all | solution.py:49
  368.9 71.6 %all-to-all-start.3 = ((f32[4,192,768]{2,1,0:T(8,128)}), f32[4,192,768]{2,1,0:T(8,128)}, u32[]{:S(2)}, u32[]{:S(2)}) async-start(f32[4,192,768]{2,1,0:T(8,128)} %bitcast.22), calls=%async_computation.3 | async-start | bytes 4718592 | tf_op jit(solution)/shard_map/all_to_all | solution.py:49
  440.5 71.4 %all-to-all-start.5 = ((f32[4,192,768]{2,1,0:T(8,128)}), f32[4,192,768]{2,1,0:T(8,128)}, u32[]{:S(2)}, u32[]{:S(2)}) async-start(f32[4,192,768]{2,1,0:T(8,128)} %bitcast.21), calls=%async_computation.5 | async-start | bytes 4718592 | tf_op jit(solution)/shard_map/all_to_all | solution.py:49
Sparse Core Ops, SparseCore 0:
  8.9 59.7 all-gather.2
  76.0 50.1 all-gather.4
